TPU v7x, 32 devices: a whole 2x2x4 slice. The times are simulated.
32 devices in a mesh: pages: 8 (over y, x, core), heads: 4 (over z).
Axes of the slice: x: 2, y: 2, z: 4, core: 2. Of those that a mesh axis runs over, the one named last changes fastest.
Arguments:
- queries: bfloat16 [512, 32, 128], P('pages', 'heads'), may hold values from -6 to 6
- keys: bfloat16 [576, 16, 128, 128], P('pages', 'heads'), may hold values from -6 to 6
- values: bfloat16 [576, 16, 128, 128], P('pages', 'heads'), may hold values from -6 to 6
- hot_pages: int32 [64], replicated, may hold values from 0 to 575, as said below
- hot_used: int32 [512], replicated, may hold values from 1 to 64
- user_pages: int32 [512, 1], P('pages'), may hold values from 8 to 71, as said below
- lengths: int32 [512], P('pages'), may hold values from 1 to 128
- o_weight: bfloat16 [4096, 4608], P('heads'), may hold values from -0.09375 to 0.09375
- residual: bfloat16 [512, 4608], P(('pages', 'heads')), may hold values from -6 to 6
- norm_gain: float32 [4608], replicated, may hold values from 0.25 to 1.75
Outputs:
- output: bfloat16 [512, 4608], P(('pages', 'heads'))
Inputs may be any that keep to these rules, and one draw needn't show every extreme that they name: `hot_pages`: 64 distinct pages; each lies among the first 8 pages of its group (page p belongs to group p // 72); one group holds exactly 8 of them and none holds more. `user_pages`: numbers within the sequence's own group (sequence s belongs to group s // 64); all own pages of the sequences of one group are distinct.
All inputs are finite; a program needn't handle non-finite values.
Results may differ from a plain program's by a relative error of at most 0.019.
Values may be sent and summed in bfloat16 or wider, within the bound.
No kernel may reach another device: no remote copies, remote signals or barrier semaphores. Data moves between devices by JAX's collectives and lax.ppermute only.
A program may use at most 128 MiB of HBM per device.

v0:
```python
import jax
import jax.numpy as jnp
from jax import lax
from jax.sharding import PartitionSpec as P

HOT_CAP = 8
score_scale = 1.0 / 12.0
soft_cap = 50.0
epsilon = 1e-06


def shared_terms(grouped, page_keys, page_values, allowed):
    logits = jnp.einsum("skgd,pktd->skgpt", grouped, page_keys, preferred_element_type=jnp.float32)
    weight = jnp.exp(soft_cap * jnp.tanh(logits * (score_scale / soft_cap)))
    weight = jnp.where(allowed[:, None, None, :, None], weight, 0.0)
    numerator = jnp.einsum(
        "skgpt,pktd->skgd",
        weight.astype(jnp.bfloat16),
        page_values,
        preferred_element_type=jnp.float32,
    )
    return (numerator, jnp.sum(weight, axis=(3, 4)))


def own_terms(grouped, owned_keys, owned_values, lengths):
    logits = jnp.einsum(
        "skgd,suktd->skgut", grouped, owned_keys, preferred_element_type=jnp.float32
    )
    page_len = owned_keys.shape[3]
    token_pos = (
        jnp.arange(owned_keys.shape[1], dtype=jnp.int32)[:, None] * page_len
        + jnp.arange(page_len, dtype=jnp.int32)[None, :]
    )
    allowed = token_pos[None, :, :] < lengths[:, None, None]
    weight = jnp.exp(soft_cap * jnp.tanh(logits * (score_scale / soft_cap)))
    weight = jnp.where(allowed[:, None, None, :, :], weight, 0.0)
    numerator = jnp.einsum(
        "skgut,suktd->skgd",
        weight.astype(jnp.bfloat16),
        owned_values,
        preferred_element_type=jnp.float32,
    )
    return (numerator, jnp.sum(weight, axis=(3, 4)))


def slot_places(page_ids, hot_pages):
    hot_order = jnp.arange(hot_pages.shape[0], dtype=jnp.int32)
    matches = page_ids[:, None] == hot_pages[None, :]
    present = jnp.any(matches, axis=1)
    position = jnp.sum(jnp.where(matches, hot_order[None, :], 0), axis=1)
    return (present, position)


def per_device(
    queries, keys, values, hot_pages, hot_used, user_pages, lengths, o_weight, residual, norm_gain
):
    seq_dev, head_count, head_dim = queries.shape
    kv_heads = keys.shape[1]
    group_size = head_count // kv_heads
    page_count = keys.shape[0]
    grouped = queries.reshape(seq_dev, kv_heads, group_size, head_dim)
    myself = lax.axis_index("pages")
    hot_keys = keys[:HOT_CAP]
    hot_values = values[:HOT_CAP]
    everyone = lax.all_gather(queries, "pages", axis=0, tiled=True)
    page_ids = myself * page_count + jnp.arange(HOT_CAP, dtype=jnp.int32)
    present, position = slot_places(page_ids, hot_pages)
    allowed = present[None, :] & (position[None, :] < hot_used[:, None])
    everyone_grouped = everyone.reshape(everyone.shape[0], kv_heads, group_size, head_dim)
    numerator, totals = shared_terms(everyone_grouped, hot_keys, hot_values, allowed)
    numerator, totals = (
        lax.psum_scatter(
            numerator.astype(jnp.bfloat16), "pages", scatter_dimension=0, tiled=True
        ).astype(jnp.float32),
        lax.psum_scatter(
            totals.astype(jnp.bfloat16), "pages", scatter_dimension=0, tiled=True
        ).astype(jnp.float32),
    )
    owned_keys = keys[user_pages]
    owned_values = values[user_pages]
    own_numerator, own_totals = own_terms(grouped, owned_keys, owned_values, lengths)
    attended = ((numerator + own_numerator) / (totals + own_totals)[:, :, :, None]).astype(
        jnp.bfloat16
    )
    attended = attended.reshape(seq_dev, head_count * head_dim)
    projected = lax.psum_scatter(
        jnp.dot(attended, o_weight, preferred_element_type=jnp.float32).astype(jnp.bfloat16),
        "heads",
        scatter_dimension=0,
        tiled=True,
    ).astype(jnp.float32)
    mean_sq = jnp.mean(projected * projected, axis=1, keepdims=True)
    normed = projected / jnp.sqrt(mean_sq + epsilon) * norm_gain[None, :]
    return (residual.astype(jnp.float32) + normed).astype(jnp.bfloat16)


def solution(mesh):
    in_specs = (
        P("pages", "heads", None),
        P("pages", "heads", None, None),
        P("pages", "heads", None, None),
        P(),
        P(),
        P("pages", None),
        P("pages"),
        P("heads", None),
        P(("pages", "heads"), None),
        P(),
    )
    out_specs = P(("pages", "heads"), None)
    return jax.shard_map(
        per_device, mesh=mesh, in_specs=in_specs, out_specs=out_specs, check_vma=False
    )
```

profile of v0, /device:TPU:0, one launch (start us, length us, event | category | flops | bytes accessed | tf_op | source)
XLA Modules:
  0.0 159.2 jit_solution(6237646934203751264)
XLA Ops:
  6.5 0.7 all-gather.2.cloned.1.call-update
  7.3 0.0 reduce-scatter.10.cloned.1.call-start
  7.3 0.7 fusion.27
  8.0 9.2 %gather_fusion = bf16[64,4,128,128]{3,2,1,0:T(8,128)(2,1)} fusion(bf16[72,4,128,128]{3,2,1,0:T(8,128)(2,1)} %param.11, s32[1024]{0:T(1024)S(1)} %pad_clamp_fusion), kind=kCustom, calls=%fused_computation | custom fusion | bytes 16777472 | tf_op jit(solution)/shard_map/gather | solution.py:79
  17.2 9.4 %gather_fusion.1 = bf16[64,4,128,128]{3,2,1,0:T(8,128)(2,1)} fusion(bf16[72,4,128,128]{3,2,1,0:T(8,128)(2,1)} %param.12, s32[1024]{0:T(1024)S(1)} %pad_clamp_fusion), kind=kCustom, calls=%fused_computation.1 | custom fusion | bytes 16777472 | tf_op jit(solution)/shard_map/gather | solution.py:80
  26.6 0.2 compare_reduce_fusion
  26.8 0.2 fusion.26
  26.9 0.1 compare_and_fusion
  27.0 8.3 %all-gather.2.cloned.1.call-done = bf16[512,8,128]{2,1,0:T(8,128)(2,1)} async-done(((bf16[64,8,128]{2,1,0:T(8,128)(2,1)}), bf16[512,8,128]{2,1,0:T(8,128)(2,1)}) %all-gather.2.cloned.1.call-update) | async-done | bytes 1048592 | tf_op jit(solution)/shard_map/all_gather | solution.py:65
  35.3 1.4 copy.39
  36.7 9.5 %fusion = (bf16[512,4,2]{0,2,1:T(2,128)(2,1)S(1)}, f32[4,8,128,512,2]{3,2,4,1,0:T(8,128)}) fusion(pred[512,8]{0,1:T(8,128)(4,1)S(1)} %compare_and_fusion, bf16[512,4,2,128,1]{3,0,2,4,1:T(8,128)(2,1)S(1)} %bitcast.55, bf16[72,4,128,128]{3,2,1,0:T(8,128)(2,1)} %param.11), kind=kOutput, calls=%fused_computation.3 | convolution fusion | flops 1090514944 | bytes 18886656 | tf_op jit(solution)/shard_map/skgd,pktd->skgpt/dot_general | solution.py:13
  46.2 0.8 copy.55
  47.0 0.0 reduce-scatter.10.cloned.1.call-update
  47.0 0.0 reduce-scatter.6.cloned.1.call-start
  47.1 10.1 %fusion.7 = bf16[512,4,2,128]{3,0,2,1:T(8,128)(2,1)} fusion(f32[4,8,128,512,2]{3,2,4,1,0:T(8,128)} %get-tuple-element.8, pred[512,8]{0,1:T(8,128)(4,1)S(1)} %compare_and_fusion, bf16[72,4,128,128]{3,2,1,0:T(8,128)(2,1)} %param.12), kind=kOutput, calls=%fused_computation.9 | convolution fusion | flops 1091043328 | bytes 18878464 | tf_op jit(solution)/shard_map/skgpt,pktd->skgd/dot_general | solution.py:16
  57.2 0.0 reduce-scatter.6.cloned.1.call-update
  57.2 0.2 reduce-scatter.8.cloned.1.call-start
  57.5 0.1 iota_compare_fusion
  57.5 8.0 %fusion.31 = (f32[64,4,2]{2,1,0:T(4,128)S(1)}, bf16[64,4,2,128]{3,2,1,0:T(2,128)(2,1)S(1)}) fusion(bf16[64,4,128,128]{3,2,1,0:T(8,128)(2,1)} %gather_fusion, bf16[64,4,2,128]{3,2,1,0:T(2,128)(2,1)S(1)} %bitcast.56, pred[64,128]{1,0:T(8,128)(4,1)S(1)} %iota_compare_fusion), kind=kOutput, calls=%fused_computation.45 | convolution fusion | flops 17104384 | bytes 8660992 | tf_op jit(solution)/shard_map/skgd,suktd->skgut/dot_general | solution.py:26
  65.5 0.1 copy.44
  65.6 5.7 %fusion.24 = f32[64,4,2,128]{3,2,1,0:T(2,128)S(1)} fusion(bf16[64,4,128,128]{3,2,1,0:T(8,128)(2,1)} %gather_fusion.1, bf16[64,4,2,128]{3,2,1,0:T(2,128)(2,1)S(1)} %get-tuple-element.6), kind=kOutput, calls=%fused_computation.29 | convolution fusion | flops 16777216 | bytes 8781824 | tf_op jit(solution)/shard_map/skgut,suktd->skgd/dot_general | solution.py:37
  71.3 9.6 %reduce-scatter.10.cloned.1.call-done = bf16[64,8]{1,0:T(8,128)(2,1)} async-done(((bf16[512,8]{1,0:T(8,128)(2,1)}), bf16[64,8]{1,0:T(8,128)(2,1)}) %reduce-scatter.10.cloned.1.call-update) | async-done | bytes 1040
  80.9 0.8 copy.56
  81.7 38.4 %reduce-scatter.6.cloned.1.call-done = bf16[64,4,2,128]{3,0,2,1:T(8,128)(2,1)} async-done(((bf16[512,4,2,128]{3,0,2,1:T(8,128)(2,1)}), bf16[64,4,2,128]{3,0,2,1:T(8,128)(2,1)}) %reduce-scatter.6.cloned.1.call-update) | async-done | bytes 131088 | tf_op jit(solution)/shard_map/reduce_scatter | solution.py:72
  120.1 1.0 fusion.23
  121.1 0.1 copy.46
  121.3 0.1 reshape.104
  121.3 6.2 %convolution_convert_fusion = bf16[64,4608]{1,0:T(8,128)(2,1)} fusion(bf16[64,1024]{1,0:T(8,128)(2,1)S(1)} %reshape.104, bf16[1024,4608]{1,0:T(8,128)(2,1)} %param.17), kind=kOutput, calls=%fused_computation.7 | convolution fusion | flops 604274688 | bytes 10158080 | tf_op jit(solution)/shard_map/dot_general | solution.py:87
  127.6 0.0 reduce-scatter.8.cloned.1.call-update
  127.6 22.3 %reduce-scatter.8.cloned.1.call-done = bf16[16,4608]{1,0:T(8,128)(2,1)} async-done(((bf16[64,4608]{1,0:T(8,128)(2,1)}), bf16[16,4608]{1,0:T(8,128)(2,1)}) %reduce-scatter.8.cloned.1.call-update) | async-done | bytes 147472 | tf_op jit(solution)/shard_map/reduce_scatter | solution.py:86
  149.9 1.1 fusion.18
  151.0 1.7 %fusion.21 = bf16[16,4608]{1,0:T(8,128)(2,1)} fusion(bf16[16,4608]{1,0:T(8,128)(2,1)} %reduce-scatter.8.cloned.1.call-done, bf16[16,4608]{1,0:T(8,128)(2,1)S(1)} %copy-done, f32[4608]{0:T(1024)S(1)} %copy-done.2, f32[16]{0:T(128)S(1)} %add_sqrt_fusion), kind=kLoop, calls=%fused_computation.25 | loop fusion | flops 442368 | bytes 460864 | tf_op jit(solution)/shard_map/convert_element_type | solution.py:94
  (19 shorter events, 0.1 us)
Async XLA Ops:
  6.5 28.8 %all-gather.2.cloned.1.call-start = ((), (), s32[]{:S(2)}) async-start(), calls=%async_computation.3 | async-start | bytes 1179648 | tf_op jit(solution)/shard_map/all_gather | solution.py:65
  7.3 73.7 %reduce-scatter.10.cloned.1.call-start = ((), (), s32[]{:S(2)}) async-start(), calls=%async_computation.6 | async-start | bytes 147456
  17.2 9.4 %copy-start.5 = (s32[64]{0:T(128)S(1)}, s32[64]{0:T(128)}, u32[]{:S(2)}) copy-start(s32[64]{0:T(128)} %param.13) | copy-start | bytes 772
  17.2 9.8 %copy-start.3 = (s32[512]{0:T(512)S(1)}, s32[512]{0:T(512)}, u32[]{:S(2)}) copy-start(s32[512]{0:T(512)} %param.14) | copy-start | bytes 6148
  47.0 73.0 %reduce-scatter.6.cloned.1.call-start = ((), (), s32[]{:S(2)}) async-start(), calls=%async_computation.4 | async-start | bytes 1179648 | tf_op jit(solution)/shard_map/reduce_scatter | solution.py:72
  47.1 10.4 %copy-start.4 = (s32[64]{0:T(128)S(1)}, s32[64]{0:T(128)}, u32[]{:S(2)}) copy-start(s32[64]{0:T(128)} %param.16) | copy-start | bytes 772
  47.1 10.4 %copy-start.1 = (bf16[64,8,128]{2,1,0:T(8,128)(2,1)S(1)}, bf16[64,8,128]{2,1,0:T(8,128)(2,1)}, u32[]{:S(2)}) copy-start(bf16[64,8,128]{2,1,0:T(8,128)(2,1)} %param.10) | copy-start | bytes 393220
  57.2 92.7 %reduce-scatter.8.cloned.1.call-start = ((), (), s32[]{:S(2)}) async-start(), calls=%async_computation.5 | async-start | bytes 737280 | tf_op jit(solution)/shard_map/reduce_scatter | solution.py:86
  71.3 79.7 %copy-start = (bf16[16,4608]{1,0:T(8,128)(2,1)S(1)}, bf16[16,4608]{1,0:T(8,128)(2,1)}, u32[]{:S(2)}) copy-start(bf16[16,4608]{1,0:T(8,128)(2,1)} %param.18) | copy-start | bytes 442372
  71.3 79.7 %copy-start.2 = (f32[4608]{0:T(1024)S(1)}, f32[4608]{0:T(1024)}, u32[]{:S(2)}) copy-start(f32[4608]{0:T(1024)} %param.19) | copy-start | bytes 55300
Sparse Core Ops, SparseCore 0:
  9.2 26.0 all-gather.1
  47.2 33.6 reduce-scatter.9
  84.1 35.9 reduce-scatter.5
  127.7 22.1 reduce-scatter.7
where the time goes:
time: 160 us; the launch traced here: 159 us
  waiting for transfers between devices  79.3 us (50%)
  matrix products  39.5 us (25%)
  local copies, waits for them, and re-layouts  21.9 us (14%)
  between operations  13.2 us (8%)
  other arithmetic  5 us (3%)
    reduce_scatter x1, waiting for transfers between devices, per_device(): lax.psum_scatter(numerator.astype(jnp.bfloat16), 'pages', scatter_dimensi...  38.4 us
    reduce_scatter x1, waiting for transfers between devices, per_device(): lax.psum_scatter(jnp.dot(attended, o_weight, preferred_element_type=jnp.f...  22.3 us
    unnamed x5, waiting for transfers between devices  10.3 us
    dot_general x1, matrix products, shared_terms(): jnp.einsum('skgpt,pktd->skgd', weight.astype(jnp.bfloat16), page_values,...  10.1 us
    dot_general x1, matrix products, shared_terms(): jnp.einsum('skgd,pktd->skgpt', grouped, page_keys, preferred_element_type...  9.5 us
    gather x1, local copies, waits for them, and re-layouts, per_device(): owned_values = values[user_pages]  9.39 us
    gather x1, local copies, waits for them, and re-layouts, per_device(): owned_keys = keys[user_pages]  9.2 us
    all_gather x1, waiting for transfers between devices, per_device(): everyone = lax.all_gather(queries, 'pages', axis=0, tiled=True)  8.32 us
  transfers between devices with their start and end apart: 4, of which 4 were waited for; matrix products, arithmetic and copies ran while one was open for 28% of the time, Pallas kernels for 0%

commit v1 on v0

--- a/solution.py
+++ b/solution.py
@@ -54,6 +54,29 @@
 def per_device(
     queries, keys, values, hot_pages, hot_used, user_pages, lengths, o_weight, residual, norm_gain
 ):
+
+    def joints_form(chunk):
+        response, part_now, low = (lax.psum(1, "pages"), lax.axis_index("pages"), chunk.shape[0])
+        runs = [(to_i, (to_i + 1) % response) for to_i in range(response)]
+        rows = [(to_i, (to_i - 1) % response) for to_i in range(response)]
+        after = jnp.zeros((*chunk.shape[:0], response * low, *chunk.shape[1:]), chunk.dtype)
+        after = lax.dynamic_update_slice_in_dim(after, chunk, part_now * low, axis=0)
+        found_now = z_new = chunk
+        row_out = response // 2
+        i0 = 1
+        while i0 < row_out + 1:
+            found_now = lax.ppermute(found_now, "pages", runs)
+            after = lax.dynamic_update_slice_in_dim(
+                after, found_now, (part_now - i0) % response * low, axis=0
+            )
+            if i0 < response - row_out:
+                z_new = lax.ppermute(z_new, "pages", rows)
+                after = lax.dynamic_update_slice_in_dim(
+                    after, z_new, (part_now + i0) % response * low, axis=0
+                )
+            i0 += 1
+        return after
+
     seq_dev, head_count, head_dim = queries.shape
     kv_heads = keys.shape[1]
     group_size = head_count // kv_heads
@@ -62,7 +85,7 @@
     myself = lax.axis_index("pages")
     hot_keys = keys[:HOT_CAP]
     hot_values = values[:HOT_CAP]
-    everyone = lax.all_gather(queries, "pages", axis=0, tiled=True)
+    everyone = joints_form(queries)
     page_ids = myself * page_count + jnp.arange(HOT_CAP, dtype=jnp.int32)
     present, position = slot_places(page_ids, hot_pages)
     allowed = present[None, :] & (position[None, :] < hot_used[:, None])

time: 160 us -> 173 us (1.081)
  starting transfers between devices: 0.31 us -> 8.92 us
  waiting for transfers between devices: 79.3 us -> 83.4 us
    ppermute x0 -> x7, waiting for transfers between devices: none -> 10.6 us  [the longest x4 10.6 us: joints_form(): found_now = lax.ppermute(found_now, 'pages', runs)]
    ppermute x0 -> x7, starting transfers between devices: none -> 8.65 us  [the longest x3 8.14 us: joints_form(): z_new = lax.ppermute(z_new, 'pages', rows)]
    all_gather x1 -> x0, waiting for transfers between devices: 8.32 us -> none  [per_device(): everyone = lax.all_gather(queries, 'pages', axis=0, tiled=True)]
    unnamed x5 -> x4, waiting for transfers between devices: 10.3 us -> 12.1 us
  transfers between devices with their start and end apart: 4 -> 10, of which waited for: 4 -> 6; matrix products, arithmetic and copies ran while one was open for 28% -> 27% of each run, Pallas kernels for 0% -> 0%
where the time goes in v1:
time: 173 us; the launch traced here: 172 us
  waiting for transfers between devices  83.4 us (48%)
  matrix products  39.5 us (23%)
  local copies, waits for them, and re-layouts  20.8 us (12%)
  between operations  13.3 us (8%)
  starting transfers between devices  8.92 us (5%)
  other arithmetic  6.31 us (4%)
    reduce_scatter x1, waiting for transfers between devices, per_device(): lax.psum_scatter(numerator.astype(jnp.bfloat16), 'pages', scatter_dimensi...  38.4 us
    reduce_scatter x1, waiting for transfers between devices, per_device(): lax.psum_scatter(jnp.dot(attended, o_weight, preferred_element_type=jnp.f...  22.3 us
    unnamed x4, waiting for transfers between devices  12.1 us
    ppermute x4, waiting for transfers between devices, joints_form(): found_now = lax.ppermute(found_now, 'pages', runs)  10.6 us
    dot_general x1, matrix products, shared_terms(): jnp.einsum('skgpt,pktd->skgd', weight.astype(jnp.bfloat16), page_values,...  10.1 us
    dot_general x1, matrix products, shared_terms(): jnp.einsum('skgd,pktd->skgpt', grouped, page_keys, preferred_element_type...  9.51 us
    gather x1, local copies, waits for them, and re-layouts, per_device(): owned_keys = keys[user_pages]  9.23 us
    gather x1, local copies, waits for them, and re-layouts, per_device(): owned_values = values[user_pages]  9.21 us
  transfers between devices with their start and end apart: 10, of which 6 were waited for; matrix products, arithmetic and copies ran while one was open for 27% of the time, Pallas kernels for 0%

profile of v1, /device:TPU:0, one launch (start us, length us, event | category | flops | bytes accessed | tf_op | source)
XLA Modules:
  0.0 172.2 jit_solution(1971294753507689)
XLA Ops:
  6.5 0.5 collective-permute-start
  7.0 2.9 %collective-permute-start.1 = (bf16[64,8,128]{2,1,0:T(8,128)(2,1)}, bf16[64,8,128]{2,1,0:T(8,128)(2,1)S(1)}, u32[]{:S(2)}, u32[]{:S(2)}) collective-permute-start(bf16[64,8,128]{2,1,0:T(8,128)(2,1)} %param.10), channel_id=1, source_target_pairs={{0,28},{4,0},{8,4},{12,8},{16,12},{20,16},{24,20},{28,24},{1,29},{... | collective-permute-start | bytes 393224 | tf_op jit(solution)/shard_map/ppermute | solution.py:73
  9.9 0.8 fusion.17
  10.7 0.8 compare_reduce_fusion
  11.6 0.7 fusion.18
  12.3 9.2 %gather_fusion.1 = bf16[64,4,128,128]{3,2,1,0:T(8,128)(2,1)} fusion(bf16[72,4,128,128]{3,2,1,0:T(8,128)(2,1)} %param.12, s32[1024]{0:T(1024)S(1)} %pad_clamp_fusion), kind=kCustom, calls=%fused_computation.1 | custom fusion | bytes 16777472 | tf_op jit(solution)/shard_map/gather | solution.py:103
  21.5 9.2 %gather_fusion = bf16[64,4,128,128]{3,2,1,0:T(8,128)(2,1)} fusion(bf16[72,4,128,128]{3,2,1,0:T(8,128)(2,1)} %param.11, s32[1024]{0:T(1024)S(1)} %pad_clamp_fusion), kind=kCustom, calls=%fused_computation | custom fusion | bytes 16777472 | tf_op jit(solution)/shard_map/gather | solution.py:102
  30.7 0.1 broadcast_in_dim.58
  30.9 0.1 compare_and_fusion
  31.0 2.6 %collective-permute-start.3 = (bf16[64,8,128]{2,1,0:T(8,128)(2,1)S(1)}, bf16[64,8,128]{2,1,0:T(8,128)(2,1)S(1)}, u32[]{:S(2)}, u32[]{:S(2)}) collective-permute-start(bf16[64,8,128]{2,1,0:T(8,128)(2,1)S(1)} %collective-permute-done.1), channel_id=1, source_target_pairs={{0,28},{4,0},{8,4},{12,8},{16,12},{20,16},{24,20},{28,24},{1,29},{... | collective-permute-start | bytes 393224 | tf_op jit(solution)/shard_map/ppermute | solution.py:73
  33.7 2.6 %collective-permute-done.2 = bf16[64,8,128]{2,1,0:T(8,128)(2,1)S(1)} collective-permute-done((bf16[64,8,128]{2,1,0:T(8,128)(2,1)S(1)}, bf16[64,8,128]{2,1,0:T(8,128)(2,1)S(1)}, u32[]{:S(2)}, u32[]{:S(2)}) %collective-permute-start.2) | collective-permute-done | bytes 131104 | tf_op jit(solution)/shard_map/ppermute | solution.py:68
  36.3 2.6 %collective-permute-start.5 = (bf16[64,8,128]{2,1,0:T(8,128)(2,1)S(1)}, bf16[64,8,128]{2,1,0:T(8,128)(2,1)S(1)}, u32[]{:S(2)}, u32[]{:S(2)}) collective-permute-start(bf16[64,8,128]{2,1,0:T(8,128)(2,1)S(1)} %collective-permute-done.3), channel_id=1, source_target_pairs={{0,28},{4,0},{8,4},{12,8},{16,12},{20,16},{24,20},{28,24},{1,29},{... | collective-permute-start | bytes 393224 | tf_op jit(solution)/shard_map/ppermute | solution.py:73
  39.0 2.9 %collective-permute-done.4 = bf16[64,8,128]{2,1,0:T(8,128)(2,1)S(1)} collective-permute-done((bf16[64,8,128]{2,1,0:T(8,128)(2,1)S(1)}, bf16[64,8,128]{2,1,0:T(8,128)(2,1)S(1)}, u32[]{:S(2)}, u32[]{:S(2)}) %collective-permute-start.4) | collective-permute-done | bytes 131104 | tf_op jit(solution)/shard_map/ppermute | solution.py:68
  42.0 5.2 %collective-permute-done.6 = bf16[64,8,128]{2,1,0:T(8,128)(2,1)S(1)} collective-permute-done((bf16[64,8,128]{2,1,0:T(8,128)(2,1)S(1)}, bf16[64,8,128]{2,1,0:T(8,128)(2,1)S(1)}, u32[]{:S(2)}, u32[]{:S(2)}) %collective-permute-start.6) | collective-permute-done | bytes 131104 | tf_op jit(solution)/shard_map/ppermute | solution.py:68
  47.2 9.5 %bitcast_reduce_fusion = (bf16[512,4,2]{0,2,1:T(2,128)(2,1)S(1)}, f32[4,512,2,8,128]{1,4,3,2,0:T(8,128)}) fusion(pred[512,8]{0,1:T(8,128)(4,1)S(1)} %compare_and_fusion, bf16[512,4,2,128,1]{3,0,4,2,1:T(8,128)(2,1)S(1)} %bitcast.48, bf16[72,4,128,128]{3,2,1,0:T(8,128)(2,1)} %param.11), kind=kOutput, calls=%fused_computation.2 | convolution fusion | flops 1090514944 | bytes 18886656 | tf_op jit(solution)/shard_map/skgd,pktd->skgpt/dot_general | solution.py:13
  56.7 0.8 copy.89
  57.6 10.1 %fusion.2 = bf16[512,4,2,128]{3,0,2,1:T(8,128)(2,1)} fusion(f32[4,512,2,8,128]{1,4,3,2,0:T(8,128)} %get-tuple-element.8, pred[512,8]{0,1:T(8,128)(4,1)S(1)} %compare_and_fusion, bf16[72,4,128,128]{3,2,1,0:T(8,128)(2,1)} %param.12), kind=kOutput, calls=%fused_computation.9 | convolution fusion | flops 1091043328 | bytes 18878464 | tf_op jit(solution)/shard_map/skgpt,pktd->skgd/dot_general | solution.py:16
  67.7 0.2 reduce-scatter.8.cloned.1.call-start
  68.0 0.1 iota_compare_fusion
  68.0 8.0 %fusion.22 = (f32[64,4,2]{2,1,0:T(4,128)S(1)}, bf16[64,4,2,128]{3,2,1,0:T(2,128)(2,1)S(1)}) fusion(bf16[64,4,128,128]{3,2,1,0:T(8,128)(2,1)} %gather_fusion, bf16[64,4,2,128]{3,2,1,0:T(2,128)(2,1)S(1)} %bitcast.49, pred[64,128]{1,0:T(8,128)(4,1)S(1)} %iota_compare_fusion), kind=kOutput, calls=%fused_computation.52 | convolution fusion | flops 17104384 | bytes 8660992 | tf_op jit(solution)/shard_map/skgd,suktd->skgut/dot_general | solution.py:26
  76.1 0.1 copy.79
  76.2 5.7 %fusion.15 = f32[64,4,2,128]{3,2,1,0:T(2,128)S(1)} fusion(bf16[64,4,128,128]{3,2,1,0:T(8,128)(2,1)} %gather_fusion.1, bf16[64,4,2,128]{3,2,1,0:T(2,128)(2,1)S(1)} %get-tuple-element.6), kind=kOutput, calls=%fused_computation.36 | convolution fusion | flops 16777216 | bytes 8781824 | tf_op jit(solution)/shard_map/skgut,suktd->skgd/dot_general | solution.py:37
  81.8 12.0 %reduce-scatter.10.cloned.1.call-done = bf16[64,8]{1,0:T(8,128)(2,1)} async-done(((bf16[512,8]{1,0:T(8,128)(2,1)}), bf16[64,8]{1,0:T(8,128)(2,1)}) %reduce-scatter.10.cloned.1.call-update) | async-done | bytes 1040
  93.9 0.8 copy.90
  94.7 38.4 %reduce-scatter.6.cloned.1.call-done = bf16[64,4,2,128]{3,0,2,1:T(8,128)(2,1)} async-done(((bf16[512,4,2,128]{3,0,2,1:T(8,128)(2,1)}), bf16[64,4,2,128]{3,0,2,1:T(8,128)(2,1)}) %reduce-scatter.6.cloned.1.call-update) | async-done | bytes 131088 | tf_op jit(solution)/shard_map/reduce_scatter | solution.py:95
  133.0 1.0 fusion.14
  134.1 0.1 copy.81
  134.2 0.1 reshape.104
  134.3 6.2 %convolution_convert_fusion = bf16[64,4608]{1,0:T(8,128)(2,1)} fusion(bf16[64,1024]{1,0:T(8,128)(2,1)S(1)} %reshape.104, bf16[1024,4608]{1,0:T(8,128)(2,1)} %param.17), kind=kOutput, calls=%fused_computation.7 | convolution fusion | flops 604274688 | bytes 10158080 | tf_op jit(solution)/shard_map/dot_general | solution.py:110
  140.6 22.3 %reduce-scatter.8.cloned.1.call-done = bf16[16,4608]{1,0:T(8,128)(2,1)} async-done(((bf16[64,4608]{1,0:T(8,128)(2,1)}), bf16[16,4608]{1,0:T(8,128)(2,1)}) %reduce-scatter.8.cloned.1.call-update) | async-done | bytes 147472 | tf_op jit(solution)/shard_map/reduce_scatter | solution.py:109
  162.8 1.1 fusion.9
  163.9 1.7 fusion.12
  (36 shorter events, 0.5 us)
Async XLA Ops:
  6.5 87.3 %reduce-scatter.10.cloned.1.call-start = ((), (), s32[]{:S(2)}) async-start(), calls=%async_computation.5 | async-start | bytes 147456
  6.5 24.4 %collective-permute-start = (bf16[64,8,128]{2,1,0:T(8,128)(2,1)}, bf16[64,8,128]{2,1,0:T(8,128)(2,1)S(1)}, u32[]{:S(2)}, u32[]{:S(2)}) collective-permute-start(bf16[64,8,128]{2,1,0:T(8,128)(2,1)} %param.10), channel_id=1, source_target_pairs={{0,4},{4,8},{8,12},{12,16},{16,20},{20,24},{24,28},{28,0},{1,5},{5... | collective-permute-start | bytes 393224 | tf_op jit(solution)/shard_map/ppermute | solution.py:68
  7.0 24.0 %collective-permute-start.1 = (bf16[64,8,128]{2,1,0:T(8,128)(2,1)}, bf16[64,8,128]{2,1,0:T(8,128)(2,1)S(1)}, u32[]{:S(2)}, u32[]{:S(2)}) collective-permute-start(bf16[64,8,128]{2,1,0:T(8,128)(2,1)} %param.10), channel_id=1, source_target_pairs={{0,28},{4,0},{8,4},{12,8},{16,12},{20,16},{24,20},{28,24},{1,29},{... | collective-permute-start | bytes 393224 | tf_op jit(solution)/shard_map/ppermute | solution.py:73
  21.5 9.4 %copy-start.1 = (bf16[64,8,128]{2,1,0:T(8,128)(2,1)S(1)}, bf16[64,8,128]{2,1,0:T(8,128)(2,1)}, u32[]{:S(2)}) copy-start(bf16[64,8,128]{2,1,0:T(8,128)(2,1)} %param.10) | copy-start | bytes 393220
  21.5 9.4 %copy-start.3 = (s32[512]{0:T(512)S(1)}, s32[512]{0:T(512)}, u32[]{:S(2)}) copy-start(s32[512]{0:T(512)} %param.14) | copy-start | bytes 6148
  31.0 5.3 %collective-permute-start.2 = (bf16[64,8,128]{2,1,0:T(8,128)(2,1)S(1)}, bf16[64,8,128]{2,1,0:T(8,128)(2,1)S(1)}, u32[]{:S(2)}, u32[]{:S(2)}) collective-permute-start(bf16[64,8,128]{2,1,0:T(8,128)(2,1)S(1)} %collective-permute-done), channel_id=1, source_target_pairs={{0,4},{4,8},{8,12},{12,16},{16,20},{20,24},{24,28},{28,0},{1,5},{5... | collective-permute-start | bytes 393224 | tf_op jit(solution)/shard_map/ppermute | solution.py:68
  31.0 5.3 %collective-permute-start.3 = (bf16[64,8,128]{2,1,0:T(8,128)(2,1)S(1)}, bf16[64,8,128]{2,1,0:T(8,128)(2,1)S(1)}, u32[]{:S(2)}, u32[]{:S(2)}) collective-permute-start(bf16[64,8,128]{2,1,0:T(8,128)(2,1)S(1)} %collective-permute-done.1), channel_id=1, source_target_pairs={{0,28},{4,0},{8,4},{12,8},{16,12},{20,16},{24,20},{28,24},{1,29},{... | collective-permute-start | bytes 393224 | tf_op jit(solution)/shard_map/ppermute | solution.py:73
  36.3 5.6 %collective-permute-start.4 = (bf16[64,8,128]{2,1,0:T(8,128)(2,1)S(1)}, bf16[64,8,128]{2,1,0:T(8,128)(2,1)S(1)}, u32[]{:S(2)}, u32[]{:S(2)}) collective-permute-start(bf16[64,8,128]{2,1,0:T(8,128)(2,1)S(1)} %collective-permute-done.2), channel_id=1, source_target_pairs={{0,4},{4,8},{8,12},{12,16},{16,20},{20,24},{24,28},{28,0},{1,5},{5... | collective-permute-start | bytes 393224 | tf_op jit(solution)/shard_map/ppermute | solution.py:68
  36.3 5.6 %collective-permute-start.5 = (bf16[64,8,128]{2,1,0:T(8,128)(2,1)S(1)}, bf16[64,8,128]{2,1,0:T(8,128)(2,1)S(1)}, u32[]{:S(2)}, u32[]{:S(2)}) collective-permute-start(bf16[64,8,128]{2,1,0:T(8,128)(2,1)S(1)} %collective-permute-done.3), channel_id=1, source_target_pairs={{0,28},{4,0},{8,4},{12,8},{16,12},{20,16},{24,20},{28,24},{1,29},{... | collective-permute-start | bytes 393224 | tf_op jit(solution)/shard_map/ppermute | solution.py:73
  41.9 5.3 %collective-permute-start.6 = (bf16[64,8,128]{2,1,0:T(8,128)(2,1)S(1)}, bf16[64,8,128]{2,1,0:T(8,128)(2,1)S(1)}, u32[]{:S(2)}, u32[]{:S(2)}) collective-permute-start(bf16[64,8,128]{2,1,0:T(8,128)(2,1)S(1)} %collective-permute-done.4), channel_id=1, source_target_pairs={{0,4},{4,8},{8,12},{12,16},{16,20},{20,24},{24,28},{28,0},{1,5},{5... | collective-permute-start | bytes 393224 | tf_op jit(solution)/shard_map/ppermute | solution.py:68
  57.6 75.5 %reduce-scatter.6.cloned.1.call-start = ((), (), s32[]{:S(2)}) async-start(), calls=%async_computation.3 | async-start | bytes 1179648 | tf_op jit(solution)/shard_map/reduce_scatter | solution.py:95
  57.6 10.3 %copy-start.4 = (s32[64]{0:T(128)S(1)}, s32[64]{0:T(128)}, u32[]{:S(2)}) copy-start(s32[64]{0:T(128)} %param.16) | copy-start | bytes 772
  67.7 95.1 %reduce-scatter.8.cloned.1.call-start = ((), (), s32[]{:S(2)}) async-start(), calls=%async_computation.4 | async-start | bytes 737280 | tf_op jit(solution)/shard_map/reduce_scatter | solution.py:109
  81.8 82.1 %copy-start = (bf16[16,4608]{1,0:T(8,128)(2,1)S(1)}, bf16[16,4608]{1,0:T(8,128)(2,1)}, u32[]{:S(2)}) copy-start(bf16[16,4608]{1,0:T(8,128)(2,1)} %param.18) | copy-start | bytes 442372
  81.8 82.1 %copy-start.2 = (f32[4608]{0:T(1024)S(1)}, f32[4608]{0:T(1024)}, u32[]{:S(2)}) copy-start(f32[4608]{0:T(1024)} %param.19) | copy-start | bytes 55300
Sparse Core Ops, SparseCore 0:
  57.7 36.1 reduce-scatter.9
  97.0 35.9 reduce-scatter.5
  140.7 22.1 reduce-scatter.7
